TPU v7x, 32 devices: a whole 2x2x4 slice. The times are simulated.
32 devices in a mesh: gx: 4 (over y, core), gy: 8 (over z, x).
Axes of the slice: x: 2, y: 2, z: 4, core: 2. Of those that a mesh axis runs over, the one named last changes fastest.
Arguments:
- right_side: float32 [128, 256, 512], P('gx', 'gy'), as said below
- start_guess: float32 [128, 256, 512], P('gx', 'gy'), may hold values from -3 to 3
- conductivity: float32 [128, 256, 512], P('gx', 'gy'), may hold values from 0.5 to 8
Outputs:
- solution_field: float32 [128, 256, 512], P('gx', 'gy')
- estimate: float32 [], replicated
Inputs may be any that keep to these rules, and one draw needn't show every extreme that they name: `right_side`: A smoothly varying positive scale times noise, which may have a nonzero mean.
All inputs are finite; a program needn't handle non-finite values.
Results may differ from a plain program's by a relative error of at most 0.0003.
Values sent between devices are 32-bit elements; how exact they have to be, the bound alone decides.
No kernel may reach another device: no remote copies, remote signals or barrier semaphores. Data moves between devices by JAX's collectives and lax.ppermute only.
A program may use at most 64 MiB of HBM per device.

v0:
```python
import jax
import jax.numpy as jnp
from jax import lax
from jax.sharding import PartitionSpec as P

M = 3


def with_halo(cells, sides, width):
    for axis, dim in sides:
        count = lax.axis_size(axis)
        ends = count - 1
        head = lax.slice_in_dim(cells, 0, width, axis=dim)
        tail = lax.slice_in_dim(cells, cells.shape[dim] - width, cells.shape[dim], axis=dim)
        cells = jnp.concatenate(
            [
                lax.ppermute(tail, axis, [(i, (i + 1) % count) for i in range(ends)]),
                cells,
                lax.ppermute(head, axis, [((i + 1) % count, i) for i in range(ends)]),
            ],
            axis=dim,
        )
    return cells


def shifted(padded, which, sign):
    starts = [1, 1, 1]
    starts[which] = 1 + sign
    limits = [starts[dim] + padded.shape[dim] - 2 for dim in range(3)]
    return lax.slice(padded, starts, limits)


def extend_z(padded):
    return jnp.pad(padded, ((0, 0), (0, 0), (1, 1)))


def stencil(field, kappa_pad):
    padded = extend_z(with_halo(field, (("gx", 0), ("gy", 1)), 1))
    centre = shifted(padded, 0, 0)
    middle = shifted(kappa_pad, 0, 0)
    result = jnp.zeros_like(centre)
    for which in range(3):
        for sign in (-1, 1):
            result = result + 0.5 * (middle + shifted(kappa_pad, which, sign)) * (
                centre - shifted(padded, which, sign)
            )
    return result


def global_norm(vector):
    return jnp.sqrt(lax.psum(jnp.sum(vector * vector), ("gx", "gy")))


def least_squares(columns, beta):
    count = len(columns)
    rhs_vals = [beta] + [jnp.float32(0.0)] * count
    cosines = []
    sines = []
    upper = []
    for column in range(count):
        entries = list(columns[column])
        for earlier in range(column):
            first = entries[earlier]
            second = entries[earlier + 1]
            entries[earlier] = cosines[earlier] * first + sines[earlier] * second
            entries[earlier + 1] = -sines[earlier] * first + cosines[earlier] * second
        first = entries[column]
        second = entries[column + 1]
        radius = jnp.sqrt(first * first + second * second)
        cosines.append(first / radius)
        sines.append(second / radius)
        entries[column] = radius
        rhs_vals[column + 1] = -sines[column] * rhs_vals[column]
        rhs_vals[column] = cosines[column] * rhs_vals[column]
        upper.append(entries[: column + 1])
    coeffs = [None] * count
    for row in reversed(range(count)):
        value = rhs_vals[row]
        for later in range(row + 1, count):
            value = value - upper[later][row] * coeffs[later]
        coeffs[row] = value / upper[row][row]
    return (coeffs, jnp.abs(rhs_vals[count]))


def local(right_side, start_guess, conductivity):
    kappa_pad = extend_z(with_halo(conductivity, (("gx", 0), ("gy", 1)), 1))
    start = right_side - stencil(start_guess, kappa_pad)
    beta = global_norm(start)
    basis = [start / beta]
    columns = []
    for column in range(M):
        vector = stencil(basis[column], kappa_pad)
        local_dots = jnp.stack([jnp.sum(vector * basis[earlier]) for earlier in range(column + 1)])
        coeff_all, squares = lax.psum((local_dots, jnp.sum(vector * vector)), ("gx", "gy"))
        for earlier in range(column + 1):
            vector = vector - coeff_all[earlier] * basis[earlier]
        entries = [coeff_all[earlier] for earlier in range(column + 1)]
        length = jnp.sqrt(squares - jnp.sum(coeff_all * coeff_all))
        entries.append(length)
        columns.append(entries)
        basis.append(vector / length)
    coeffs, estimate = least_squares(columns, beta)
    solution_field = start_guess
    for column in range(M):
        solution_field = solution_field + coeffs[column] * basis[column]
    return (solution_field, estimate)


def solution(mesh):
    in_specs = (P("gx", "gy", None), P("gx", "gy", None), P("gx", "gy", None))
    out_specs = (P("gx", "gy", None), P())
    return jax.shard_map(local, mesh=mesh, in_specs=in_specs, out_specs=out_specs, check_vma=False)
```

profile of v0, /device:TPU:0, one launch (start us, length us, event | category | flops | bytes accessed | tf_op | source)
XLA Modules:
  0.0 344.9 jit_solution(8450779061837298228)
XLA Ops:
  1.6 2.4 collective-permute-start
  6.3 5.2 %collective-permute-start.1 = (f32[1,32,512]{2,0,1:T(1,128)S(1)}, f32[1,32,512]{2,0,1:T(1,128)S(1)}, u32[]{:S(2)}, u32[]{:S(2)}) collective-permute-start(f32[1,32,512]{2,0,1:T(1,128)S(1)} %copy.8), channel_id=1, source_target_pairs={{0,8},{8,16},{16,24},{1,9},{9,17},{17,25},{2,10},{10,18},{18,26},{... | collective-permute-start | bytes 196616 | tf_op jit(solution)/shard_map/ppermute | solution.py:17
  13.0 2.8 copy.7
  17.1 3.4 collective-permute-start.4
  21.9 4.6 %collective-permute-start.5 = (f32[34,1,512]{2,0,1:T(8,128)S(1)}, f32[34,1,512]{2,0,1:T(8,128)S(1)}, u32[]{:S(2)}, u32[]{:S(2)}) collective-permute-start(f32[34,1,512]{2,0,1:T(8,128)S(1)} %get-tuple-element.31), channel_id=1, source_target_pairs={{0,1},{1,2},{2,3},{3,4},{4,5},{5,6},{6,7},{8,9},{9,10},{10,11},{11... | collective-permute-start | bytes 208904 | tf_op jit(solution)/shard_map/ppermute | solution.py:17
  27.8 3.1 select_maximum_fusion.16
  30.9 2.4 collective-permute-done.7
  33.3 3.0 select_maximum_fusion.12
  36.4 9.9 %multiply_reduce_fusion.9 = (f32[]{:T(128)}, f32[32,32,512]{2,0,1:T(8,128)}) fusion(f32[32,32,512]{2,0,1:T(8,128)S(1)} %copy.28, f32[34,34,514]{2,0,1:T(8,128)S(1)} %select_maximum_fusion.12, f32[32,32,512]{2,0,1:T(8,128)S(1)} %copy.7, f32[34,34,514]{2,0,1:T(8,128)S(1)} %select_maximum_fusion.16, f32[34,1,512]{2,0,1:T(8,128)S(1)} %collective-permute-done.7, ...), kind=kLoop, calls=%fused_computation.156 | loop fusion | flops 25165824 | bytes 17317892 | tf_op jit(solution)/shard_map/reduce_sum | solution.py:51
  46.3 44.5 %psum.49 = f32[]{:T(128)} all-reduce(f32[]{:T(128)} %get-tuple-element.21), channel_id=1, replica_groups=mesh['gx'=4,'gy'=8] {'gx','gy'}, use_global_device_ids=true, to_apply=%region_1.2 | all-reduce | flops 1 | bytes 8 | tf_op jit(solution)/shard_map/psum | solution.py:51
  96.0 4.5 %collective-permute-done.9 = f32[1,32,512]{2,0,1:T(1,128)S(1)} collective-permute-done((f32[1,32,512]{2,0,1:T(1,128)S(1)}, f32[1,32,512]{2,0,1:T(1,128)S(1)}, u32[]{:S(2)}, u32[]{:S(2)}) %collective-permute-start.9) | collective-permute-done | bytes 65568 | tf_op jit(solution)/shard_map/ppermute | solution.py:19
  100.6 2.0 collective-permute-start.10
  104.7 4.5 %collective-permute-done.11 = f32[34,1,512]{2,0,1:T(8,128)S(1)} collective-permute-done((f32[34,1,512]{2,0,1:T(8,128)S(1)}, f32[34,1,512]{2,0,1:T(8,128)S(1)}, u32[]{:S(2)}, u32[]{:S(2)}) %collective-permute-start.11) | collective-permute-done | bytes 69664 | tf_op jit(solution)/shard_map/ppermute | solution.py:19
  109.1 3.0 select_maximum_fusion.8
  112.2 8.3 %multiply_reduce_fusion.8 = (f32[]{:T(128)}, f32[]{:T(128)}, f32[32,32,512]{2,0,1:T(8,128)}) fusion(f32[32,32,512]{2,0,1:T(8,128)S(1)} %broadcast_divide_fusion, f32[34,34,514]{2,0,1:T(8,128)S(1)} %select_maximum_fusion.8, f32[32,32,512]{2,0,1:T(8,128)S(1)} %copy-done.5, f32[34,34,514]{2,0,1:T(8,128)S(1)} %select_maximum_fusion.16, ...), kind=kLoop, calls=%fused_computation.155 | loop fusion | flops 25690112 | bytes 15220744 | tf_op jit(solution)/shard_map/reduce_sum | solution.py:93
  120.5 42.9 %all-reduce.7 = (f32[]{:T(128)}, f32[1]{0:T(128)}) all-reduce(f32[]{:T(128)} %get-tuple-element.12, f32[1]{0:T(128)} %bitcast), channel_id=1, replica_groups=mesh['gx'=4,'gy'=8] {'gx','gy'}, use_global_device_ids=true, to_apply=%region_5.6 | all-reduce | flops 2 | bytes 16 | tf_op jit(solution)/shard_map/psum | solution.py:94
  165.4 3.4 subtract_divide_fusion.1
  171.5 4.6 %collective-permute-done.13 = f32[1,32,512]{2,0,1:T(1,128)S(1)} collective-permute-done((f32[1,32,512]{2,0,1:T(1,128)S(1)}, f32[1,32,512]{2,0,1:T(1,128)S(1)}, u32[]{:S(2)}, u32[]{:S(2)}) %collective-permute-start.13) | collective-permute-done | bytes 65568 | tf_op jit(solution)/shard_map/ppermute | solution.py:19
  176.2 2.0 collective-permute-start.14
  180.2 4.6 %collective-permute-done.15 = f32[34,1,512]{2,0,1:T(8,128)S(1)} collective-permute-done((f32[34,1,512]{2,0,1:T(8,128)S(1)}, f32[34,1,512]{2,0,1:T(8,128)S(1)}, u32[]{:S(2)}, u32[]{:S(2)}) %collective-permute-start.15) | collective-permute-done | bytes 69664 | tf_op jit(solution)/shard_map/ppermute | solution.py:19
  184.8 3.0 select_maximum_fusion.4
  187.9 8.6 %multiply_reduce_fusion.6 = (f32[]{:T(128)}, f32[]{:T(128)}, f32[]{:T(128)}, f32[32,32,512]{2,0,1:T(8,128)}) fusion(f32[32,32,512]{2,0,1:T(8,128)S(1)} %subtract_divide_fusion.1, f32[34,34,514]{2,0,1:T(8,128)S(1)} %select_maximum_fusion.4, f32[32,32,512]{2,0,1:T(8,128)S(1)} %copy-done.6, f32[34,34,514]{2,0,1:T(8,128)S(1)} %select_maximum_fusion.16, ...), kind=kLoop, calls=%fused_computation.152 | loop fusion | flops 27262976 | bytes 17317904 | tf_op jit(solution)/shard_map/reduce_sum | solution.py:93
  197.9 42.9 %all-reduce.6 = (f32[]{:T(128)}, f32[2]{0:T(128)S(1)}) all-reduce(f32[]{:T(128)} %get-tuple-element.9, f32[2]{0:T(128)S(1)} %pad_maximum_fusion.55), channel_id=1, replica_groups=mesh['gx'=4,'gy'=8] {'gx','gy'}, use_global_device_ids=true, to_apply=%region_10.11 | all-reduce | flops 3 | bytes 24 | tf_op jit(solution)/shard_map/psum | solution.py:94
  243.6 5.0 %subtract_divide_fusion = f32[32,32,512]{2,0,1:T(8,128)S(1)} fusion(f32[32,32,512]{2,0,1:T(8,128)} %copy-done, f32[32,32,512]{2,0,1:T(8,128)} %get-tuple-element.19, f32[]{:T(128)S(6)} %sqrt.24, f32[]{:T(128)} %bitcast.6, f32[]{:T(128)} %bitcast.5, f32[32,32,512]{2,0,1:T(8,128)} %get-tuple-element.22, f32[]{:T(128)S(6)} %sqrt.21), kind=kLoop, calls=%fused_computation.149 | loop fusion | flops 3145728 | bytes 8388624 | tf_op jit(solution)/shard_map/div | solution.py:101
  251.3 4.6 %collective-permute-done.17 = f32[1,32,512]{2,0,1:T(1,128)S(1)} collective-permute-done((f32[1,32,512]{2,0,1:T(1,128)S(1)}, f32[1,32,512]{2,0,1:T(1,128)S(1)}, u32[]{:S(2)}, u32[]{:S(2)}) %collective-permute-start.17) | collective-permute-done | bytes 65568 | tf_op jit(solution)/shard_map/ppermute | solution.py:19
  256.6 2.6 collective-permute-start.18
  265.9 4.6 %select_maximum_fusion = f32[34,34,514]{2,0,1:T(8,128)S(1)} fusion(f32[34,1,512]{2,0,1:T(8,128)} %collective-permute-done.19, f32[34,1,512]{2,0,1:T(8,128)} %collective-permute-done.18, f32[1,32,512]{2,0,1:T(1,128)} %copy-done.24, f32[32,32,512]{2,0,1:T(8,128)} %copy-done.7, f32[1,32,512]{2,0,1:T(1,128)} %copy-done.22), kind=kLoop, calls=%fused_computation.2 | loop fusion | flops 7130208 | bytes 4744224 | tf_op jit(solution)/shard_map/concatenate | solution.py:15
  270.5 14.5 %multiply_reduce_fusion = (f32[]{:T(128)}, f32[]{:T(128)}, f32[]{:T(128)}, f32[]{:T(128)}) fusion(f32[32,32,512]{2,0,1:T(8,128)} %copy-done.7, f32[32,32,512]{2,0,1:T(8,128)S(1)} %copy-done.1, f32[34,34,514]{2,0,1:T(8,128)S(1)} %select_maximum_fusion, f32[32,32,512]{2,0,1:T(8,128)} %copy-done.4, f32[34,34,514]{2,0,1:T(8,128)S(1)} %select_maximum_fusion.16, ...), kind=kLoop, calls=%fused_computation.145 | loop fusion | flops 28311552 | bytes 17317908 | tf_op jit(solution)/shard_map/reduce_sum | solution.py:94
  285.0 1.9 pad_maximum_fusion.56
  286.9 42.5 %all-reduce.5 = (f32[3]{0:T(128)S(1)}, f32[]{:T(128)}) all-reduce(f32[3]{0:T(128)S(1)} %pad_maximum_fusion.56, f32[]{:T(128)} %get-tuple-element.4), channel_id=1, replica_groups=mesh['gx'=4,'gy'=8] {'gx','gy'}, use_global_device_ids=true, to_apply=%region_15.16 | all-reduce | flops 4 | bytes 32 | tf_op jit(solution)/shard_map/psum | solution.py:94
  335.9 5.4 %multiply_add_fusion = f32[32,32,512]{2,0,1:T(8,128)S(1)} fusion(f32[32,32,512]{2,0,1:T(8,128)} %copy-done.7, f32[32,32,512]{2,0,1:T(8,128)} %copy-done, f32[]{:T(128)S(6)} %div.56, f32[]{:T(128)S(6)} %div.57, f32[]{:T(128)S(6)} %div.58, f32[32,32,512]{2,1,0:T(8,128)} %param.4, f32[32,32,512]{2,0,1:T(8,128)} %get-tuple-element.22, f32[]{:T(128)S(6)} %sqrt.21), kind=kLoop, calls=%fused_computation.144 | loop fusion | flops 3670016 | bytes 10485776 | tf_op jit(solution)/shard_map/add | solution.py:105
  341.3 2.5 copy.29
  (100 shorter events, 29.2 us)
Async XLA Ops:
  1.6 15.5 %collective-permute-start = (f32[1,32,512]{2,0,1:T(1,128)S(1)}, f32[1,32,512]{2,0,1:T(1,128)S(1)}, u32[]{:S(2)}, u32[]{:S(2)}) collective-permute-start(f32[1,32,512]{2,0,1:T(1,128)S(1)} %copy.5), channel_id=1, source_target_pairs={{0,8},{8,16},{16,24},{1,9},{9,17},{17,25},{2,10},{10,18},{18,26},{... | collective-permute-start | bytes 196616 | tf_op jit(solution)/shard_map/ppermute | solution.py:17
  4.1 13.0 %collective-permute-start.2 = (f32[1,32,512]{2,0,1:T(1,128)S(1)}, f32[1,32,512]{2,0,1:T(1,128)S(1)}, u32[]{:S(2)}, u32[]{:S(2)}) collective-permute-start(f32[1,32,512]{2,0,1:T(1,128)S(1)} %copy.11), channel_id=1, source_target_pairs={{8,0},{16,8},{24,16},{9,1},{17,9},{25,17},{10,2},{18,10},{26,18},{... | collective-permute-start | bytes 196616 | tf_op jit(solution)/shard_map/ppermute | solution.py:19
  6.3 15.5 %collective-permute-start.1 = (f32[1,32,512]{2,0,1:T(1,128)S(1)}, f32[1,32,512]{2,0,1:T(1,128)S(1)}, u32[]{:S(2)}, u32[]{:S(2)}) collective-permute-start(f32[1,32,512]{2,0,1:T(1,128)S(1)} %copy.8), channel_id=1, source_target_pairs={{0,8},{8,16},{16,24},{1,9},{9,17},{17,25},{2,10},{10,18},{18,26},{... | collective-permute-start | bytes 196616 | tf_op jit(solution)/shard_map/ppermute | solution.py:17
  11.6 10.3 %collective-permute-start.3 = (f32[1,32,512]{2,0,1:T(1,128)S(1)}, f32[1,32,512]{2,0,1:T(1,128)S(1)}, u32[]{:S(2)}, u32[]{:S(2)}) collective-permute-start(f32[1,32,512]{2,0,1:T(1,128)S(1)} %copy.14), channel_id=1, source_target_pairs={{8,0},{16,8},{24,16},{9,1},{17,9},{25,17},{10,2},{18,10},{26,18},{... | collective-permute-start | bytes 196616 | tf_op jit(solution)/shard_map/ppermute | solution.py:19
  15.8 20.5 %copy-start.4 = (f32[32,32,512]{2,0,1:T(8,128)}, f32[32,32,512]{2,0,1:T(8,128)S(1)}, u32[]{:S(2)}) copy-start(f32[32,32,512]{2,0,1:T(8,128)S(1)} %copy.7) | copy-start | bytes 6291460
  17.1 19.2 %copy-start.9 = (f32[1,32,512]{2,0,1:T(1,128)}, f32[1,32,512]{2,0,1:T(1,128)S(1)}, u32[]{:S(2)}) copy-start(f32[1,32,512]{2,0,1:T(1,128)S(1)} %collective-permute-done.2) | copy-start | bytes 196612
  17.1 10.6 %collective-permute-start.4 = (f32[34,1,512]{2,0,1:T(8,128)S(1)}, f32[34,1,512]{2,0,1:T(8,128)S(1)}, u32[]{:S(2)}, u32[]{:S(2)}) collective-permute-start(f32[34,1,512]{2,0,1:T(8,128)S(1)} %get-tuple-element.29), channel_id=1, source_target_pairs={{0,1},{1,2},{2,3},{3,4},{4,5},{5,6},{6,7},{8,9},{9,10},{10,11},{11... | collective-permute-start | bytes 208904 | tf_op jit(solution)/shard_map/ppermute | solution.py:17
  20.6 7.2 %collective-permute-start.6 = (f32[34,1,512]{2,0,1:T(8,128)S(1)}, f32[34,1,512]{2,0,1:T(8,128)S(1)}, u32[]{:S(2)}, u32[]{:S(2)}) collective-permute-start(f32[34,1,512]{2,0,1:T(8,128)S(1)} %get-tuple-element.30), channel_id=1, source_target_pairs={{1,0},{2,1},{3,2},{4,3},{5,4},{6,5},{7,6},{9,8},{10,9},{11,10},{12... | collective-permute-start | bytes 208904 | tf_op jit(solution)/shard_map/ppermute | solution.py:19
  21.9 9.0 %collective-permute-start.5 = (f32[34,1,512]{2,0,1:T(8,128)S(1)}, f32[34,1,512]{2,0,1:T(8,128)S(1)}, u32[]{:S(2)}, u32[]{:S(2)}) collective-permute-start(f32[34,1,512]{2,0,1:T(8,128)S(1)} %get-tuple-element.31), channel_id=1, source_target_pairs={{0,1},{1,2},{2,3},{3,4},{4,5},{5,6},{6,7},{8,9},{9,10},{10,11},{11... | collective-permute-start | bytes 208904 | tf_op jit(solution)/shard_map/ppermute | solution.py:17
  26.5 6.8 %collective-permute-start.7 = (f32[34,1,512]{2,0,1:T(8,128)S(1)}, f32[34,1,512]{2,0,1:T(8,128)S(1)}, u32[]{:S(2)}, u32[]{:S(2)}) collective-permute-start(f32[34,1,512]{2,0,1:T(8,128)S(1)} %get-tuple-element.32), channel_id=1, source_target_pairs={{1,0},{2,1},{3,2},{4,3},{5,4},{6,5},{7,6},{9,8},{10,9},{11,10},{12... | collective-permute-start | bytes 208904 | tf_op jit(solution)/shard_map/ppermute | solution.py:19
  93.4 2.6 collective-permute-start.8
  94.7 5.8 %collective-permute-start.9 = (f32[1,32,512]{2,0,1:T(1,128)S(1)}, f32[1,32,512]{2,0,1:T(1,128)S(1)}, u32[]{:S(2)}, u32[]{:S(2)}) collective-permute-start(f32[1,32,512]{2,0,1:T(1,128)S(1)} %get-tuple-element.38), channel_id=1, source_target_pairs={{8,0},{16,8},{24,16},{9,1},{17,9},{25,17},{10,2},{18,10},{26,18},{... | collective-permute-start | bytes 196616 | tf_op jit(solution)/shard_map/ppermute | solution.py:19
  100.6 4.1 %collective-permute-start.10 = (f32[34,1,512]{2,0,1:T(8,128)S(1)}, f32[34,1,512]{2,0,1:T(8,128)S(1)}, u32[]{:S(2)}, u32[]{:S(2)}) collective-permute-start(f32[34,1,512]{2,0,1:T(8,128)S(1)} %get-tuple-element.27), channel_id=1, source_target_pairs={{0,1},{1,2},{2,3},{3,4},{4,5},{5,6},{6,7},{8,9},{9,10},{10,11},{11... | collective-permute-start | bytes 208904 | tf_op jit(solution)/shard_map/ppermute | solution.py:17
  102.6 9.6 %copy-start.5 = (f32[32,32,512]{2,0,1:T(8,128)S(1)}, f32[32,32,512]{2,0,1:T(8,128)}, u32[]{:S(2)}) copy-start(f32[32,32,512]{2,0,1:T(8,128)} %copy-done.4) | copy-start | bytes 6291460
  102.6 9.6 %copy-start.10 = (f32[1,32,512]{2,0,1:T(1,128)S(1)}, f32[1,32,512]{2,0,1:T(1,128)}, u32[]{:S(2)}) copy-start(f32[1,32,512]{2,0,1:T(1,128)} %copy-done.9) | copy-start | bytes 196612
  102.6 9.6 %copy-start.15 = (f32[34,1,512]{2,0,1:T(8,128)S(1)}, f32[34,1,512]{2,0,1:T(8,128)}, u32[]{:S(2)}) copy-start(f32[34,1,512]{2,0,1:T(8,128)} %copy-done.14) | copy-start | bytes 208900
  102.7 9.6 %copy-start.19 = (f32[34,1,512]{2,0,1:T(8,128)S(1)}, f32[34,1,512]{2,0,1:T(8,128)}, u32[]{:S(2)}) copy-start(f32[34,1,512]{2,0,1:T(8,128)} %copy-done.18) | copy-start | bytes 208900
  102.7 6.5 %collective-permute-start.11 = (f32[34,1,512]{2,0,1:T(8,128)S(1)}, f32[34,1,512]{2,0,1:T(8,128)S(1)}, u32[]{:S(2)}, u32[]{:S(2)}) collective-permute-start(f32[34,1,512]{2,0,1:T(8,128)S(1)} %get-tuple-element.28), channel_id=1, source_target_pairs={{1,0},{2,1},{3,2},{4,3},{5,4},{6,5},{7,6},{9,8},{10,9},{11,10},{12... | collective-permute-start | bytes 208904 | tf_op jit(solution)/shard_map/ppermute | solution.py:19
  168.8 19.0 %copy-start = (f32[32,32,512]{2,0,1:T(8,128)}, f32[32,32,512]{2,0,1:T(8,128)S(1)}, u32[]{:S(2)}) copy-start(f32[32,32,512]{2,0,1:T(8,128)S(1)} %subtract_divide_fusion.1) | copy-start | bytes 6291460
  168.9 2.6 collective-permute-start.12
  170.2 5.9 %collective-permute-start.13 = (f32[1,32,512]{2,0,1:T(1,128)S(1)}, f32[1,32,512]{2,0,1:T(1,128)S(1)}, u32[]{:S(2)}, u32[]{:S(2)}) collective-permute-start(f32[1,32,512]{2,0,1:T(1,128)S(1)} %get-tuple-element.36), channel_id=1, source_target_pairs={{8,0},{16,8},{24,16},{9,1},{17,9},{25,17},{10,2},{18,10},{26,18},{... | collective-permute-start | bytes 196616 | tf_op jit(solution)/shard_map/ppermute | solution.py:19
  176.2 4.0 %collective-permute-start.14 = (f32[34,1,512]{2,0,1:T(8,128)S(1)}, f32[34,1,512]{2,0,1:T(8,128)S(1)}, u32[]{:S(2)}, u32[]{:S(2)}) collective-permute-start(f32[34,1,512]{2,0,1:T(8,128)S(1)} %get-tuple-element.25), channel_id=1, source_target_pairs={{0,1},{1,2},{2,3},{3,4},{4,5},{5,6},{6,7},{8,9},{9,10},{10,11},{11... | collective-permute-start | bytes 208904 | tf_op jit(solution)/shard_map/ppermute | solution.py:17
  178.2 9.7 %copy-start.2 = (f32[32,32,512]{2,0,1:T(8,128)S(1)}, f32[32,32,512]{2,0,1:T(8,128)}, u32[]{:S(2)}) copy-start(f32[32,32,512]{2,0,1:T(8,128)} %get-tuple-element.22) | copy-start | bytes 6291460
  178.2 9.7 %copy-start.6 = (f32[32,32,512]{2,0,1:T(8,128)S(1)}, f32[32,32,512]{2,0,1:T(8,128)}, u32[]{:S(2)}) copy-start(f32[32,32,512]{2,0,1:T(8,128)} %copy-done.4) | copy-start | bytes 6291460
  178.2 9.7 %copy-start.11 = (f32[1,32,512]{2,0,1:T(1,128)S(1)}, f32[1,32,512]{2,0,1:T(1,128)}, u32[]{:S(2)}) copy-start(f32[1,32,512]{2,0,1:T(1,128)} %copy-done.9) | copy-start | bytes 196612
  178.2 9.7 %copy-start.16 = (f32[34,1,512]{2,0,1:T(8,128)S(1)}, f32[34,1,512]{2,0,1:T(8,128)}, u32[]{:S(2)}) copy-start(f32[34,1,512]{2,0,1:T(8,128)} %copy-done.14) | copy-start | bytes 208900
  178.2 9.7 %copy-start.20 = (f32[34,1,512]{2,0,1:T(8,128)S(1)}, f32[34,1,512]{2,0,1:T(8,128)}, u32[]{:S(2)}) copy-start(f32[34,1,512]{2,0,1:T(8,128)} %copy-done.18) | copy-start | bytes 208900
  178.2 6.6 %collective-permute-start.15 = (f32[34,1,512]{2,0,1:T(8,128)S(1)}, f32[34,1,512]{2,0,1:T(8,128)S(1)}, u32[]{:S(2)}, u32[]{:S(2)}) collective-permute-start(f32[34,1,512]{2,0,1:T(8,128)S(1)} %get-tuple-element.26), channel_id=1, source_target_pairs={{1,0},{2,1},{3,2},{4,3},{5,4},{6,5},{7,6},{9,8},{10,9},{11,10},{12... | collective-permute-start | bytes 208904 | tf_op jit(solution)/shard_map/ppermute | solution.py:19
  248.7 2.6 collective-permute-start.16
  250.0 5.9 %collective-permute-start.17 = (f32[1,32,512]{2,0,1:T(1,128)S(1)}, f32[1,32,512]{2,0,1:T(1,128)S(1)}, u32[]{:S(2)}, u32[]{:S(2)}) collective-permute-start(f32[1,32,512]{2,0,1:T(1,128)S(1)} %get-tuple-element.34), channel_id=1, source_target_pairs={{8,0},{16,8},{24,16},{9,1},{17,9},{25,17},{10,2},{18,10},{26,18},{... | collective-permute-start | bytes 196616 | tf_op jit(solution)/shard_map/ppermute | solution.py:19
  256.6 9.0 %collective-permute-start.18 = (f32[34,1,512]{2,0,1:T(8,128)}, f32[34,1,512]{2,0,1:T(8,128)}, u32[]{:S(2)}, u32[]{:S(2)}) collective-permute-start(f32[34,1,512]{2,0,1:T(8,128)} %get-tuple-element.23), channel_id=1, source_target_pairs={{0,1},{1,2},{2,3},{3,4},{4,5},{5,6},{6,7},{8,9},{9,10},{10,11},{11... | collective-permute-start | bytes 208904 | tf_op jit(solution)/shard_map/ppermute | solution.py:17
  259.2 6.6 %collective-permute-start.19 = (f32[34,1,512]{2,0,1:T(8,128)}, f32[34,1,512]{2,0,1:T(8,128)}, u32[]{:S(2)}, u32[]{:S(2)}) collective-permute-start(f32[34,1,512]{2,0,1:T(8,128)} %get-tuple-element.24), channel_id=1, source_target_pairs={{1,0},{2,1},{3,2},{4,3},{5,4},{6,5},{7,6},{9,8},{10,9},{11,10},{12... | collective-permute-start | bytes 208904 | tf_op jit(solution)/shard_map/ppermute | solution.py:19
  (14 other events, 74.9 us)
where the time goes:
time: 347 us; the launch traced here: 345 us
  blocking collectives  173 us (50%)
  other arithmetic  79 us (23%)
  starting transfers between devices  39.9 us (11%)
  waiting for transfers between devices  26.3 us (8%)
  between operations  16.7 us (5%)
  local copies, waits for them, and re-layouts  10.4 us (3%)
    psum x3, blocking collectives, local(): lax.psum((local_dots, jnp.sum(vector * vector)), ('gx', 'gy'))  128 us
    psum x1, blocking collectives, global_norm(): return jnp.sqrt(lax.psum(jnp.sum(vector * vector), ('gx', 'gy')))  44.5 us
    ppermute x10, starting transfers between devices, with_halo(): lax.ppermute(tail, axis, [(i, (i + 1) % count) for i in range(ends)])  26 us
    ppermute x10, waiting for transfers between devices, with_halo(): lax.ppermute(head, axis, [((i + 1) % count, i) for i in range(ends)])  25.5 us
    reduce_sum x2, other arithmetic, local(): jnp.sum(vector * basis[earlier])  16.9 us
    concatenate x5, other arithmetic, with_halo(): jnp.concatenate([lax.ppermute(tail, axis, [(i, (i + 1) % count) for i in...  16.7 us
    reduce_sum x1, other arithmetic, local(): jnp.sum(vector * vector)  14.5 us
    ppermute x10, starting transfers between devices, with_halo(): lax.ppermute(head, axis, [((i + 1) % count, i) for i in range(ends)])  13.8 us
  transfers between devices with their start and end apart: 20, of which 9 were waited for; matrix products, arithmetic and copies ran while one was open for 2% of the time, Pallas kernels for 0%

commit v1 on v0

--- a/solution.py
+++ b/solution.py
@@ -91,7 +91,7 @@
     for column in range(M):
         vector = stencil(basis[column], kappa_pad)
         local_dots = jnp.stack([jnp.sum(vector * basis[earlier]) for earlier in range(column + 1)])
-        coeff_all, squares = lax.psum((local_dots, jnp.sum(vector * vector)), ("gx", "gy"))
+        coeff_all, squares = lax.psum(lax.psum((local_dots, jnp.sum(vector * vector)), "gy"), "gx")
         for earlier in range(column + 1):
             vector = vector - coeff_all[earlier] * basis[earlier]
         entries = [coeff_all[earlier] for earlier in range(column + 1)]

time: 347 us -> 297 us (0.86)
  blocking collectives: 173 us -> 125 us
    psum x3 -> x6, blocking collectives: 128 us -> 81 us  [the longest x3 60.1 us: local(): lax.psum((local_dots, jnp.sum(vector * vector)), 'gy')]
  transfers between devices with their start and end apart: 20 -> 20, of which waited for: 9 -> 9; matrix products, arithmetic and copies ran while one was open for 2% -> 3% of each run, Pallas kernels for 0% -> 0%
where the time goes in v1:
time: 297 us; the launch traced here: 296 us
  blocking collectives  125 us (42%)
  other arithmetic  78.6 us (26%)
  starting transfers between devices  41.3 us (14%)
  waiting for transfers between devices  23.8 us (8%)
  between operations  16.5 us (6%)
  local copies, waits for them, and re-layouts  10.3 us (3%)
    psum x3, blocking collectives, local(): lax.psum((local_dots, jnp.sum(vector * vector)), 'gy')  60.1 us
    psum x1, blocking collectives, global_norm(): return jnp.sqrt(lax.psum(jnp.sum(vector * vector), ('gx', 'gy')))  44.4 us
    ppermute x10, starting transfers between devices, with_halo(): lax.ppermute(tail, axis, [(i, (i + 1) % count) for i in range(ends)])  27.4 us
    ppermute x10, waiting for transfers between devices, with_halo(): lax.ppermute(head, axis, [((i + 1) % count, i) for i in range(ends)])  23 us
    psum x3, blocking collectives, local(): lax.psum(lax.psum((local_dots, jnp.sum(vector * vector)), 'gy'), 'gx')  20.9 us
    reduce_sum x2, other arithmetic, local(): jnp.sum(vector * basis[earlier])  17 us
    concatenate x5, other arithmetic, with_halo(): jnp.concatenate([lax.ppermute(tail, axis, [(i, (i + 1) % count) for i in...  16.7 us
    reduce_sum x1, other arithmetic, local(): jnp.sum(vector * vector)  13.9 us
  transfers between devices with their start and end apart: 20, of which 9 were waited for; matrix products, arithmetic and copies ran while one was open for 3% of the time, Pallas kernels for 0%

profile of v1, /device:TPU:0, one launch (start us, length us, event | category | flops | bytes accessed | tf_op | source)
XLA Modules:
  0.0 295.9 jit_solution(9604738409408922633)
XLA Ops:
  1.6 2.4 collective-permute-start
  6.3 5.2 %collective-permute-start.1 = (f32[1,32,512]{2,0,1:T(1,128)S(1)}, f32[1,32,512]{2,0,1:T(1,128)S(1)}, u32[]{:S(2)}, u32[]{:S(2)}) collective-permute-start(f32[1,32,512]{2,0,1:T(1,128)S(1)} %copy.8), channel_id=1, source_target_pairs={{0,8},{8,16},{16,24},{1,9},{9,17},{17,25},{2,10},{10,18},{18,26},{... | collective-permute-start | bytes 196616 | tf_op jit(solution)/shard_map/ppermute | solution.py:17
  13.0 2.8 copy.7
  17.1 3.4 %collective-permute-start.4 = (f32[34,1,512]{2,0,1:T(8,128)S(1)}, f32[34,1,512]{2,0,1:T(8,128)S(1)}, u32[]{:S(2)}, u32[]{:S(2)}) collective-permute-start(f32[34,1,512]{2,0,1:T(8,128)S(1)} %get-tuple-element.35), channel_id=1, source_target_pairs={{0,1},{1,2},{2,3},{3,4},{4,5},{5,6},{6,7},{8,9},{9,10},{10,11},{11... | collective-permute-start | bytes 208904 | tf_op jit(solution)/shard_map/ppermute | solution.py:17
  21.9 4.6 %collective-permute-start.5 = (f32[34,1,512]{2,0,1:T(8,128)S(1)}, f32[34,1,512]{2,0,1:T(8,128)S(1)}, u32[]{:S(2)}, u32[]{:S(2)}) collective-permute-start(f32[34,1,512]{2,0,1:T(8,128)S(1)} %get-tuple-element.37), channel_id=1, source_target_pairs={{0,1},{1,2},{2,3},{3,4},{4,5},{5,6},{6,7},{8,9},{9,10},{10,11},{11... | collective-permute-start | bytes 208904 | tf_op jit(solution)/shard_map/ppermute | solution.py:17
  27.8 3.0 %select_maximum_fusion.16 = f32[34,34,514]{2,0,1:T(8,128)S(1)} fusion(f32[34,1,512]{2,0,1:T(8,128)S(1)} %collective-permute-done.6, f32[34,1,512]{2,0,1:T(8,128)S(1)} %collective-permute-done.4, f32[1,32,512]{2,0,1:T(1,128)S(1)} %collective-permute-done.2, f32[32,32,512]{2,0,1:T(8,128)S(1)} %copy.7, f32[1,32,512]{2,0,1:T(1,128)S(1)} %collective-permute-done), kind=kLoop, calls=%fused_computation.18 | loop fusion | flops 7130208 | bytes 4744224 | tf_op jit(solution)/shard_map/concatenate | solution.py:15
  30.9 2.4 collective-permute-done.7
  33.3 3.0 %select_maximum_fusion.12 = f32[34,34,514]{2,0,1:T(8,128)S(1)} fusion(f32[34,1,512]{2,0,1:T(8,128)S(1)} %collective-permute-done.7, f32[34,1,512]{2,0,1:T(8,128)S(1)} %collective-permute-done.5, f32[1,32,512]{2,0,1:T(1,128)S(1)} %collective-permute-done.3, f32[32,32,512]{2,0,1:T(8,128)S(1)} %copy.28, f32[1,32,512]{2,0,1:T(1,128)S(1)} %collective-permute-done.1), kind=kLoop, calls=%fused_computation.14 | loop fusion | flops 7130208 | bytes 4744224 | tf_op jit(solution)/shard_map/concatenate | solution.py:15
  36.4 10.0 %multiply_reduce_fusion.9 = (f32[]{:T(128)}, f32[32,32,512]{2,0,1:T(8,128)}) fusion(f32[32,32,512]{2,0,1:T(8,128)S(1)} %copy.28, f32[34,34,514]{2,0,1:T(8,128)S(1)} %select_maximum_fusion.12, f32[32,32,512]{2,0,1:T(8,128)S(1)} %copy.7, f32[34,34,514]{2,0,1:T(8,128)S(1)} %select_maximum_fusion.16, f32[34,1,512]{2,0,1:T(8,128)S(1)} %collective-permute-done.7, ...), kind=kLoop, calls=%fused_computation.156 | loop fusion | flops 25165824 | bytes 17317892 | tf_op jit(solution)/shard_map/reduce_sum | solution.py:51
  46.3 44.4 %psum.91 = f32[]{:T(128)} all-reduce(f32[]{:T(128)} %get-tuple-element.27), channel_id=1, replica_groups=mesh['gx'=4,'gy'=8] {'gx','gy'}, use_global_device_ids=true, to_apply=%region_1.2 | all-reduce | flops 1 | bytes 8 | tf_op jit(solution)/shard_map/psum | solution.py:51
  96.0 4.5 %collective-permute-done.9 = f32[1,32,512]{2,0,1:T(1,128)S(1)} collective-permute-done((f32[1,32,512]{2,0,1:T(1,128)S(1)}, f32[1,32,512]{2,0,1:T(1,128)S(1)}, u32[]{:S(2)}, u32[]{:S(2)}) %collective-permute-start.9) | collective-permute-done | bytes 65568 | tf_op jit(solution)/shard_map/ppermute | solution.py:19
  104.7 4.5 %collective-permute-done.11 = f32[34,1,512]{2,0,1:T(8,128)S(1)} collective-permute-done((f32[34,1,512]{2,0,1:T(8,128)S(1)}, f32[34,1,512]{2,0,1:T(8,128)S(1)}, u32[]{:S(2)}, u32[]{:S(2)}) %collective-permute-start.11) | collective-permute-done | bytes 69664 | tf_op jit(solution)/shard_map/ppermute | solution.py:19
  109.1 3.0 %select_maximum_fusion.8 = f32[34,34,514]{2,0,1:T(8,128)S(1)} fusion(f32[34,1,512]{2,0,1:T(8,128)S(1)} %collective-permute-done.11, f32[34,1,512]{2,0,1:T(8,128)S(1)} %collective-permute-done.10, f32[1,32,512]{2,0,1:T(1,128)S(1)} %collective-permute-done.9, f32[32,32,512]{2,0,1:T(8,128)S(1)} %broadcast_divide_fusion, f32[1,32,512]{2,0,1:T(1,128)S(1)} %collective-permute-done.8), kind=kLoop, calls=%fused_computation.10 | loop fusion | flops 7130208 | bytes 4744224 | tf_op jit(solution)/shard_map/concatenate | solution.py:15
  112.2 8.4 %multiply_reduce_fusion.8 = (f32[]{:T(128)}, f32[]{:T(128)}, f32[32,32,512]{2,0,1:T(8,128)}) fusion(f32[32,32,512]{2,0,1:T(8,128)S(1)} %broadcast_divide_fusion, f32[34,34,514]{2,0,1:T(8,128)S(1)} %select_maximum_fusion.8, f32[32,32,512]{2,0,1:T(8,128)S(1)} %copy-done.5, f32[34,34,514]{2,0,1:T(8,128)S(1)} %select_maximum_fusion.16, ...), kind=kLoop, calls=%fused_computation.155 | loop fusion | flops 25690112 | bytes 15220744 | tf_op jit(solution)/shard_map/reduce_sum | solution.py:93
  120.6 20.5 %all-reduce.7 = (f32[]{:T(128)}, f32[1]{0:T(128)}) all-reduce(f32[]{:T(128)} %get-tuple-element.12, f32[1]{0:T(128)} %bitcast), channel_id=1, replica_groups=mesh['gx'=4,'gy'=8] {'gy'}, use_global_device_ids=true, to_apply=%region_6.7 | all-reduce | flops 2 | bytes 16 | tf_op jit(solution)/shard_map/psum | solution.py:94
  141.1 6.9 %all-reduce.10 = (f32[]{:T(128)}, f32[1]{0:T(128)}) all-reduce(f32[]{:T(128)} %get-tuple-element.17, f32[1]{0:T(128)} %get-tuple-element.18), channel_id=1, replica_groups=mesh['gx'=4,'gy'=8] {'gx'}, use_global_device_ids=true, to_apply=%region_7.8 | all-reduce | flops 2 | bytes 16 | tf_op jit(solution)/shard_map/psum | solution.py:94
  149.9 3.4 %subtract_divide_fusion.1 = f32[32,32,512]{2,0,1:T(8,128)S(1)} fusion(f32[32,32,512]{2,0,1:T(8,128)} %get-tuple-element.26, f32[]{:T(128)S(6)} %sqrt.22, f32[]{:T(128)} %bitcast.1, f32[32,32,512]{2,0,1:T(8,128)} %get-tuple-element.28, f32[]{:T(128)S(6)} %sqrt.21), kind=kLoop, calls=%fused_computation.153 | loop fusion | flops 2097152 | bytes 6291468 | tf_op jit(solution)/shard_map/div | solution.py:101
  157.0 3.3 %collective-permute-done.13 = f32[1,32,512]{2,0,1:T(1,128)S(1)} collective-permute-done((f32[1,32,512]{2,0,1:T(1,128)S(1)}, f32[1,32,512]{2,0,1:T(1,128)S(1)}, u32[]{:S(2)}, u32[]{:S(2)}) %collective-permute-start.13) | collective-permute-done | bytes 65568 | tf_op jit(solution)/shard_map/ppermute | solution.py:19
  163.7 4.6 %collective-permute-done.15 = f32[34,1,512]{2,0,1:T(8,128)S(1)} collective-permute-done((f32[34,1,512]{2,0,1:T(8,128)S(1)}, f32[34,1,512]{2,0,1:T(8,128)S(1)}, u32[]{:S(2)}, u32[]{:S(2)}) %collective-permute-start.15) | collective-permute-done | bytes 69664 | tf_op jit(solution)/shard_map/ppermute | solution.py:19
  168.3 3.0 %select_maximum_fusion.4 = f32[34,34,514]{2,0,1:T(8,128)S(1)} fusion(f32[34,1,512]{2,0,1:T(8,128)S(1)} %collective-permute-done.15, f32[34,1,512]{2,0,1:T(8,128)S(1)} %collective-permute-done.14, f32[1,32,512]{2,0,1:T(1,128)S(1)} %collective-permute-done.13, f32[32,32,512]{2,0,1:T(8,128)S(1)} %subtract_divide_fusion.1, ...), kind=kLoop, calls=%fused_computation.6 | loop fusion | flops 7130208 | bytes 4744224 | tf_op jit(solution)/shard_map/concatenate | solution.py:15
  171.4 8.6 %multiply_reduce_fusion.6 = (f32[]{:T(128)}, f32[]{:T(128)}, f32[]{:T(128)}, f32[32,32,512]{2,0,1:T(8,128)}) fusion(f32[32,32,512]{2,0,1:T(8,128)S(1)} %subtract_divide_fusion.1, f32[34,34,514]{2,0,1:T(8,128)S(1)} %select_maximum_fusion.4, f32[32,32,512]{2,0,1:T(8,128)S(1)} %copy-done.6, f32[34,34,514]{2,0,1:T(8,128)S(1)} %select_maximum_fusion.16, ...), kind=kLoop, calls=%fused_computation.152 | loop fusion | flops 27262976 | bytes 17317904 | tf_op jit(solution)/shard_map/reduce_sum | solution.py:93
  181.5 19.6 %all-reduce.6 = (f32[]{:T(128)}, f32[2]{0:T(128)S(1)}) all-reduce(f32[]{:T(128)} %get-tuple-element.9, f32[2]{0:T(128)S(1)} %pad_maximum_fusion.55), channel_id=1, replica_groups=mesh['gx'=4,'gy'=8] {'gy'}, use_global_device_ids=true, to_apply=%region_13.14 | all-reduce | flops 3 | bytes 24 | tf_op jit(solution)/shard_map/psum | solution.py:94
  201.0 7.0 %all-reduce.9 = (f32[]{:T(128)}, f32[2]{0:T(128)S(1)}) all-reduce(f32[]{:T(128)} %get-tuple-element.15, f32[2]{0:T(128)S(1)} %get-tuple-element.16), channel_id=1, replica_groups=mesh['gx'=4,'gy'=8] {'gx'}, use_global_device_ids=true, to_apply=%region_14.15 | all-reduce | flops 3 | bytes 24 | tf_op jit(solution)/shard_map/psum | solution.py:94
  210.7 5.0 %subtract_divide_fusion = f32[32,32,512]{2,0,1:T(8,128)S(1)} fusion(f32[32,32,512]{2,0,1:T(8,128)} %copy-done, f32[32,32,512]{2,0,1:T(8,128)} %get-tuple-element.25, f32[]{:T(128)S(6)} %sqrt.24, f32[]{:T(128)} %bitcast.6, f32[]{:T(128)} %bitcast.5, f32[32,32,512]{2,0,1:T(8,128)} %get-tuple-element.28, f32[]{:T(128)S(6)} %sqrt.21), kind=kLoop, calls=%fused_computation.149 | loop fusion | flops 3145728 | bytes 8388624 | tf_op jit(solution)/shard_map/div | solution.py:101
  219.4 3.3 %collective-permute-done.17 = f32[1,32,512]{2,0,1:T(1,128)S(1)} collective-permute-done((f32[1,32,512]{2,0,1:T(1,128)S(1)}, f32[1,32,512]{2,0,1:T(1,128)S(1)}, u32[]{:S(2)}, u32[]{:S(2)}) %collective-permute-start.17) | collective-permute-done | bytes 65568 | tf_op jit(solution)/shard_map/ppermute | solution.py:19
  223.4 2.8 collective-permute-start.18
  232.8 4.6 %select_maximum_fusion = f32[34,34,514]{2,0,1:T(8,128)S(1)} fusion(f32[34,1,512]{2,0,1:T(8,128)} %collective-permute-done.19, f32[34,1,512]{2,0,1:T(8,128)} %collective-permute-done.18, f32[1,32,512]{2,0,1:T(1,128)} %copy-done.24, f32[32,32,512]{2,0,1:T(8,128)} %copy-done.7, f32[1,32,512]{2,0,1:T(1,128)} %copy-done.22), kind=kLoop, calls=%fused_computation.2 | loop fusion | flops 7130208 | bytes 4744224 | tf_op jit(solution)/shard_map/concatenate | solution.py:15
  237.5 13.9 %multiply_reduce_fusion = (f32[]{:T(128)}, f32[]{:T(128)}, f32[]{:T(128)}, f32[]{:T(128)}) fusion(f32[32,32,512]{2,0,1:T(8,128)} %copy-done.7, f32[32,32,512]{2,0,1:T(8,128)S(1)} %copy-done.1, f32[34,34,514]{2,0,1:T(8,128)S(1)} %select_maximum_fusion, f32[32,32,512]{2,0,1:T(8,128)} %copy-done.4, f32[34,34,514]{2,0,1:T(8,128)S(1)} %select_maximum_fusion.16, ...), kind=kLoop, calls=%fused_computation.145 | loop fusion | flops 28311552 | bytes 17317908 | tf_op jit(solution)/shard_map/reduce_sum | solution.py:94
  253.4 20.1 %all-reduce.5 = (f32[3]{0:T(128)S(1)}, f32[]{:T(128)}) all-reduce(f32[3]{0:T(128)S(1)} %pad_maximum_fusion.56, f32[]{:T(128)} %get-tuple-element.4), channel_id=1, replica_groups=mesh['gx'=4,'gy'=8] {'gy'}, use_global_device_ids=true, to_apply=%region_19.20 | all-reduce | flops 4 | bytes 32 | tf_op jit(solution)/shard_map/psum | solution.py:94
  273.5 6.9 %all-reduce.8 = (f32[3]{0:T(128)S(1)}, f32[]{:T(128)}) all-reduce(f32[3]{0:T(128)S(1)} %get-tuple-element.13, f32[]{:T(128)} %get-tuple-element.14), channel_id=1, replica_groups=mesh['gx'=4,'gy'=8] {'gx'}, use_global_device_ids=true, to_apply=%region_20.21 | all-reduce | flops 4 | bytes 32 | tf_op jit(solution)/shard_map/psum | solution.py:94
  286.9 5.4 %multiply_add_fusion = f32[32,32,512]{2,0,1:T(8,128)S(1)} fusion(f32[32,32,512]{2,0,1:T(8,128)} %copy-done.7, f32[32,32,512]{2,0,1:T(8,128)} %copy-done, f32[]{:T(128)S(6)} %div.56, f32[]{:T(128)S(6)} %div.57, f32[]{:T(128)S(6)} %div.58, f32[32,32,512]{2,1,0:T(8,128)} %param.4, f32[32,32,512]{2,0,1:T(8,128)} %get-tuple-element.28, f32[]{:T(128)S(6)} %sqrt.21), kind=kLoop, calls=%fused_computation.144 | loop fusion | flops 3670016 | bytes 10485776 | tf_op jit(solution)/shard_map/add | solution.py:105
  292.3 2.5 copy.29
  (103 shorter events, 36.5 us)
Async XLA Ops:
  1.6 15.5 %collective-permute-start = (f32[1,32,512]{2,0,1:T(1,128)S(1)}, f32[1,32,512]{2,0,1:T(1,128)S(1)}, u32[]{:S(2)}, u32[]{:S(2)}) collective-permute-start(f32[1,32,512]{2,0,1:T(1,128)S(1)} %copy.5), channel_id=1, source_target_pairs={{0,8},{8,16},{16,24},{1,9},{9,17},{17,25},{2,10},{10,18},{18,26},{... | collective-permute-start | bytes 196616 | tf_op jit(solution)/shard_map/ppermute | solution.py:17
  4.1 13.0 %collective-permute-start.2 = (f32[1,32,512]{2,0,1:T(1,128)S(1)}, f32[1,32,512]{2,0,1:T(1,128)S(1)}, u32[]{:S(2)}, u32[]{:S(2)}) collective-permute-start(f32[1,32,512]{2,0,1:T(1,128)S(1)} %copy.11), channel_id=1, source_target_pairs={{8,0},{16,8},{24,16},{9,1},{17,9},{25,17},{10,2},{18,10},{26,18},{... | collective-permute-start | bytes 196616 | tf_op jit(solution)/shard_map/ppermute | solution.py:19
  6.3 15.5 %collective-permute-start.1 = (f32[1,32,512]{2,0,1:T(1,128)S(1)}, f32[1,32,512]{2,0,1:T(1,128)S(1)}, u32[]{:S(2)}, u32[]{:S(2)}) collective-permute-start(f32[1,32,512]{2,0,1:T(1,128)S(1)} %copy.8), channel_id=1, source_target_pairs={{0,8},{8,16},{16,24},{1,9},{9,17},{17,25},{2,10},{10,18},{18,26},{... | collective-permute-start | bytes 196616 | tf_op jit(solution)/shard_map/ppermute | solution.py:17
  11.6 10.3 %collective-permute-start.3 = (f32[1,32,512]{2,0,1:T(1,128)S(1)}, f32[1,32,512]{2,0,1:T(1,128)S(1)}, u32[]{:S(2)}, u32[]{:S(2)}) collective-permute-start(f32[1,32,512]{2,0,1:T(1,128)S(1)} %copy.14), channel_id=1, source_target_pairs={{8,0},{16,8},{24,16},{9,1},{17,9},{25,17},{10,2},{18,10},{26,18},{... | collective-permute-start | bytes 196616 | tf_op jit(solution)/shard_map/ppermute | solution.py:19
  15.8 20.5 %copy-start.4 = (f32[32,32,512]{2,0,1:T(8,128)}, f32[32,32,512]{2,0,1:T(8,128)S(1)}, u32[]{:S(2)}) copy-start(f32[32,32,512]{2,0,1:T(8,128)S(1)} %copy.7) | copy-start | bytes 6291460
  17.1 19.2 %copy-start.9 = (f32[1,32,512]{2,0,1:T(1,128)}, f32[1,32,512]{2,0,1:T(1,128)S(1)}, u32[]{:S(2)}) copy-start(f32[1,32,512]{2,0,1:T(1,128)S(1)} %collective-permute-done.2) | copy-start | bytes 196612
  17.1 10.6 %collective-permute-start.4 = (f32[34,1,512]{2,0,1:T(8,128)S(1)}, f32[34,1,512]{2,0,1:T(8,128)S(1)}, u32[]{:S(2)}, u32[]{:S(2)}) collective-permute-start(f32[34,1,512]{2,0,1:T(8,128)S(1)} %get-tuple-element.35), channel_id=1, source_target_pairs={{0,1},{1,2},{2,3},{3,4},{4,5},{5,6},{6,7},{8,9},{9,10},{10,11},{11... | collective-permute-start | bytes 208904 | tf_op jit(solution)/shard_map/ppermute | solution.py:17
  20.6 7.2 %collective-permute-start.6 = (f32[34,1,512]{2,0,1:T(8,128)S(1)}, f32[34,1,512]{2,0,1:T(8,128)S(1)}, u32[]{:S(2)}, u32[]{:S(2)}) collective-permute-start(f32[34,1,512]{2,0,1:T(8,128)S(1)} %get-tuple-element.36), channel_id=1, source_target_pairs={{1,0},{2,1},{3,2},{4,3},{5,4},{6,5},{7,6},{9,8},{10,9},{11,10},{12... | collective-permute-start | bytes 208904 | tf_op jit(solution)/shard_map/ppermute | solution.py:19
  21.9 9.0 %collective-permute-start.5 = (f32[34,1,512]{2,0,1:T(8,128)S(1)}, f32[34,1,512]{2,0,1:T(8,128)S(1)}, u32[]{:S(2)}, u32[]{:S(2)}) collective-permute-start(f32[34,1,512]{2,0,1:T(8,128)S(1)} %get-tuple-element.37), channel_id=1, source_target_pairs={{0,1},{1,2},{2,3},{3,4},{4,5},{5,6},{6,7},{8,9},{9,10},{10,11},{11... | collective-permute-start | bytes 208904 | tf_op jit(solution)/shard_map/ppermute | solution.py:17
  26.5 6.8 %collective-permute-start.7 = (f32[34,1,512]{2,0,1:T(8,128)S(1)}, f32[34,1,512]{2,0,1:T(8,128)S(1)}, u32[]{:S(2)}, u32[]{:S(2)}) collective-permute-start(f32[34,1,512]{2,0,1:T(8,128)S(1)} %get-tuple-element.38), channel_id=1, source_target_pairs={{1,0},{2,1},{3,2},{4,3},{5,4},{6,5},{7,6},{9,8},{10,9},{11,10},{12... | collective-permute-start | bytes 208904 | tf_op jit(solution)/shard_map/ppermute | solution.py:19
  93.4 2.6 collective-permute-start.8
  94.7 5.8 %collective-permute-start.9 = (f32[1,32,512]{2,0,1:T(1,128)S(1)}, f32[1,32,512]{2,0,1:T(1,128)S(1)}, u32[]{:S(2)}, u32[]{:S(2)}) collective-permute-start(f32[1,32,512]{2,0,1:T(1,128)S(1)} %get-tuple-element.44), channel_id=1, source_target_pairs={{8,0},{16,8},{24,16},{9,1},{17,9},{25,17},{10,2},{18,10},{26,18},{... | collective-permute-start | bytes 196616 | tf_op jit(solution)/shard_map/ppermute | solution.py:19
  100.6 4.1 %collective-permute-start.10 = (f32[34,1,512]{2,0,1:T(8,128)S(1)}, f32[34,1,512]{2,0,1:T(8,128)S(1)}, u32[]{:S(2)}, u32[]{:S(2)}) collective-permute-start(f32[34,1,512]{2,0,1:T(8,128)S(1)} %get-tuple-element.33), channel_id=1, source_target_pairs={{0,1},{1,2},{2,3},{3,4},{4,5},{5,6},{6,7},{8,9},{9,10},{10,11},{11... | collective-permute-start | bytes 208904 | tf_op jit(solution)/shard_map/ppermute | solution.py:17
  102.6 9.5 %copy-start.5 = (f32[32,32,512]{2,0,1:T(8,128)S(1)}, f32[32,32,512]{2,0,1:T(8,128)}, u32[]{:S(2)}) copy-start(f32[32,32,512]{2,0,1:T(8,128)} %copy-done.4) | copy-start | bytes 6291460
  102.7 9.5 %copy-start.10 = (f32[1,32,512]{2,0,1:T(1,128)S(1)}, f32[1,32,512]{2,0,1:T(1,128)}, u32[]{:S(2)}) copy-start(f32[1,32,512]{2,0,1:T(1,128)} %copy-done.9) | copy-start | bytes 196612
  102.7 9.5 %copy-start.15 = (f32[34,1,512]{2,0,1:T(8,128)S(1)}, f32[34,1,512]{2,0,1:T(8,128)}, u32[]{:S(2)}) copy-start(f32[34,1,512]{2,0,1:T(8,128)} %copy-done.14) | copy-start | bytes 208900
  102.7 9.5 %copy-start.19 = (f32[34,1,512]{2,0,1:T(8,128)S(1)}, f32[34,1,512]{2,0,1:T(8,128)}, u32[]{:S(2)}) copy-start(f32[34,1,512]{2,0,1:T(8,128)} %copy-done.18) | copy-start | bytes 208900
  102.7 6.5 %collective-permute-start.11 = (f32[34,1,512]{2,0,1:T(8,128)S(1)}, f32[34,1,512]{2,0,1:T(8,128)S(1)}, u32[]{:S(2)}, u32[]{:S(2)}) collective-permute-start(f32[34,1,512]{2,0,1:T(8,128)S(1)} %get-tuple-element.34), channel_id=1, source_target_pairs={{1,0},{2,1},{3,2},{4,3},{5,4},{6,5},{7,6},{9,8},{10,9},{11,10},{12... | collective-permute-start | bytes 208904 | tf_op jit(solution)/shard_map/ppermute | solution.py:19
  153.3 18.0 %copy-start = (f32[32,32,512]{2,0,1:T(8,128)}, f32[32,32,512]{2,0,1:T(8,128)S(1)}, u32[]{:S(2)}) copy-start(f32[32,32,512]{2,0,1:T(8,128)S(1)} %subtract_divide_fusion.1) | copy-start | bytes 6291460
  153.5 3.6 %collective-permute-start.12 = (f32[1,32,512]{2,0,1:T(1,128)S(1)}, f32[1,32,512]{2,0,1:T(1,128)S(1)}, u32[]{:S(2)}, u32[]{:S(2)}) collective-permute-start(f32[1,32,512]{2,0,1:T(1,128)S(1)} %get-tuple-element.41), channel_id=1, source_target_pairs={{0,8},{8,16},{16,24},{1,9},{9,17},{17,25},{2,10},{10,18},{18,26},{... | collective-permute-start | bytes 196616 | tf_op jit(solution)/shard_map/ppermute | solution.py:17
  155.7 4.6 %collective-permute-start.13 = (f32[1,32,512]{2,0,1:T(1,128)S(1)}, f32[1,32,512]{2,0,1:T(1,128)S(1)}, u32[]{:S(2)}, u32[]{:S(2)}) collective-permute-start(f32[1,32,512]{2,0,1:T(1,128)S(1)} %get-tuple-element.42), channel_id=1, source_target_pairs={{8,0},{16,8},{24,16},{9,1},{17,9},{25,17},{10,2},{18,10},{26,18},{... | collective-permute-start | bytes 196616 | tf_op jit(solution)/shard_map/ppermute | solution.py:19
  160.4 3.3 %collective-permute-start.14 = (f32[34,1,512]{2,0,1:T(8,128)S(1)}, f32[34,1,512]{2,0,1:T(8,128)S(1)}, u32[]{:S(2)}, u32[]{:S(2)}) collective-permute-start(f32[34,1,512]{2,0,1:T(8,128)S(1)} %get-tuple-element.31), channel_id=1, source_target_pairs={{0,1},{1,2},{2,3},{3,4},{4,5},{5,6},{6,7},{8,9},{9,10},{10,11},{11... | collective-permute-start | bytes 208904 | tf_op jit(solution)/shard_map/ppermute | solution.py:17
  161.7 9.7 %copy-start.2 = (f32[32,32,512]{2,0,1:T(8,128)S(1)}, f32[32,32,512]{2,0,1:T(8,128)}, u32[]{:S(2)}) copy-start(f32[32,32,512]{2,0,1:T(8,128)} %get-tuple-element.28) | copy-start | bytes 6291460
  161.7 9.7 %copy-start.6 = (f32[32,32,512]{2,0,1:T(8,128)S(1)}, f32[32,32,512]{2,0,1:T(8,128)}, u32[]{:S(2)}) copy-start(f32[32,32,512]{2,0,1:T(8,128)} %copy-done.4) | copy-start | bytes 6291460
  161.7 9.7 %copy-start.11 = (f32[1,32,512]{2,0,1:T(1,128)S(1)}, f32[1,32,512]{2,0,1:T(1,128)}, u32[]{:S(2)}) copy-start(f32[1,32,512]{2,0,1:T(1,128)} %copy-done.9) | copy-start | bytes 196612
  161.7 9.7 %copy-start.16 = (f32[34,1,512]{2,0,1:T(8,128)S(1)}, f32[34,1,512]{2,0,1:T(8,128)}, u32[]{:S(2)}) copy-start(f32[34,1,512]{2,0,1:T(8,128)} %copy-done.14) | copy-start | bytes 208900
  161.7 9.7 %copy-start.20 = (f32[34,1,512]{2,0,1:T(8,128)S(1)}, f32[34,1,512]{2,0,1:T(8,128)}, u32[]{:S(2)}) copy-start(f32[34,1,512]{2,0,1:T(8,128)} %copy-done.18) | copy-start | bytes 208900
  161.7 6.6 %collective-permute-start.15 = (f32[34,1,512]{2,0,1:T(8,128)S(1)}, f32[34,1,512]{2,0,1:T(8,128)S(1)}, u32[]{:S(2)}, u32[]{:S(2)}) collective-permute-start(f32[34,1,512]{2,0,1:T(8,128)S(1)} %get-tuple-element.32), channel_id=1, source_target_pairs={{1,0},{2,1},{3,2},{4,3},{5,4},{6,5},{7,6},{9,8},{10,9},{11,10},{12... | collective-permute-start | bytes 208904 | tf_op jit(solution)/shard_map/ppermute | solution.py:19
  215.8 3.6 %collective-permute-start.16 = (f32[1,32,512]{2,0,1:T(1,128)S(1)}, f32[1,32,512]{2,0,1:T(1,128)S(1)}, u32[]{:S(2)}, u32[]{:S(2)}) collective-permute-start(f32[1,32,512]{2,0,1:T(1,128)S(1)} %get-tuple-element.39), channel_id=1, source_target_pairs={{0,8},{8,16},{16,24},{1,9},{9,17},{17,25},{2,10},{10,18},{18,26},{... | collective-permute-start | bytes 196616 | tf_op jit(solution)/shard_map/ppermute | solution.py:17
  218.0 4.6 %collective-permute-start.17 = (f32[1,32,512]{2,0,1:T(1,128)S(1)}, f32[1,32,512]{2,0,1:T(1,128)S(1)}, u32[]{:S(2)}, u32[]{:S(2)}) collective-permute-start(f32[1,32,512]{2,0,1:T(1,128)S(1)} %get-tuple-element.40), channel_id=1, source_target_pairs={{8,0},{16,8},{24,16},{9,1},{17,9},{25,17},{10,2},{18,10},{26,18},{... | collective-permute-start | bytes 196616 | tf_op jit(solution)/shard_map/ppermute | solution.py:19
  223.4 9.1 %collective-permute-start.18 = (f32[34,1,512]{2,0,1:T(8,128)}, f32[34,1,512]{2,0,1:T(8,128)}, u32[]{:S(2)}, u32[]{:S(2)}) collective-permute-start(f32[34,1,512]{2,0,1:T(8,128)} %get-tuple-element.29), channel_id=1, source_target_pairs={{0,1},{1,2},{2,3},{3,4},{4,5},{5,6},{6,7},{8,9},{9,10},{10,11},{11... | collective-permute-start | bytes 208904 | tf_op jit(solution)/shard_map/ppermute | solution.py:17
  226.2 6.6 %collective-permute-start.19 = (f32[34,1,512]{2,0,1:T(8,128)}, f32[34,1,512]{2,0,1:T(8,128)}, u32[]{:S(2)}, u32[]{:S(2)}) collective-permute-start(f32[34,1,512]{2,0,1:T(8,128)} %get-tuple-element.30), channel_id=1, source_target_pairs={{1,0},{2,1},{3,2},{4,3},{5,4},{6,5},{7,6},{9,8},{10,9},{11,10},{12... | collective-permute-start | bytes 208904 | tf_op jit(solution)/shard_map/ppermute | solution.py:19
  (14 other events, 73.4 us)
